TPU v7x, 128 devices: a whole 4x4x4 slice. The times are simulated.
128 devices in a mesh: rows: 32 (over y, x, core), rhs: 4 (over z).
Axes of the slice: x: 4, y: 4, z: 4, core: 2. Of those that a mesh axis runs over, the one named last changes fastest.
Arguments:
- band_blocks: float32 [256, 256, 1280], P('rows'), may hold values from -12 to 12
- precond_blocks: float32 [256, 256, 256], P('rows'), may hold values from -2 to 2
- right_side: float32 [65536, 2048], P('rows', 'rhs'), may hold values from -80 to 80
Outputs:
- solution: float32 [65536, 2048], P('rows', 'rhs')
- scaled_residual: float32 [65536, 2048], P('rows', 'rhs')
- rms_history: float32 [3, 2048], P(None, 'rhs')
- overall_rms: float32 [], replicated
All inputs are finite; a program needn't handle non-finite values.
Results may differ from a plain program's by a relative error of at most 0.0003.
Values sent between devices are 32-bit elements; how exact they have to be, the bound alone decides.
A program may use at most 128 MiB of HBM per device.

v0:
```python
import jax
import jax.numpy as jnp
from jax import lax
from jax.sharding import PartitionSpec as P

ITERS = 2


def extended(block, sides, width):
    for axis, dim in sides:
        count = lax.axis_size(axis)
        forward = [(i, i + 1) for i in range(count - 1)]
        backward = [(target, source) for source, target in forward]
        low = lax.ppermute(
            lax.slice_in_dim(block, block.shape[dim] - width, None, axis=dim), axis, forward
        )
        high = lax.ppermute(lax.slice_in_dim(block, 0, width, axis=dim), axis, backward)
        block = jnp.concatenate([low, block, high], axis=dim)
    return block


def sent_to_all(array, axis):
    copies = jnp.broadcast_to(array, (lax.axis_size(axis), *array.shape))
    return lax.all_to_all(copies, axis, split_axis=0, concat_axis=0, tiled=True)


def over_copies(array, axis):
    everything = sent_to_all(array, axis)
    return jnp.sum(everything, axis=0)


def band_times(band_blocks, padded):
    block_rows = band_blocks.shape[1]
    pieces = []
    for number in range(band_blocks.shape[0]):
        window = padded[number * block_rows : (number + 5) * block_rows]
        pieces.append(
            jnp.dot(
                band_blocks[number],
                window,
                precision=lax.Precision.HIGHEST,
                preferred_element_type=jnp.float32,
            )
        )
    return jnp.concatenate(pieces, axis=0)


def precondition(precond_blocks, operand):
    shaped = operand.reshape(precond_blocks.shape[0], precond_blocks.shape[1], operand.shape[1])
    return jnp.einsum(
        "jab,jbc->jac", precond_blocks, shaped, precision=lax.Precision.HIGHEST
    ).reshape(operand.shape)


def column_squares(residual):
    partial_value = jnp.sum(residual * residual, axis=0)
    return partial_value


def shards(band_blocks, precond_blocks, right_side):
    block_rows = band_blocks.shape[1]
    solution = precondition(precond_blocks, right_side)
    sums = []
    residual = right_side
    for sweep in range(ITERS + 1):
        rimmed = extended(solution, (("rows", 0),), 2 * block_rows)
        residual = right_side - band_times(band_blocks, rimmed)
        sums.append(column_squares(residual))
        if sweep < ITERS:
            solution = solution + precondition(precond_blocks, residual)
    stacked = jnp.stack(sums)
    stacked = over_copies(stacked, "rows")
    total_rows = lax.axis_size("rows") * right_side.shape[0]
    all_columns = lax.axis_size("rhs") * right_side.shape[1]
    history = jnp.sqrt(stacked / total_rows + 1e-06)
    scaled_residual = residual / history[ITERS][None, :]
    grand_total = over_copies(jnp.sum(stacked[ITERS]), "rhs")
    overall_rms = jnp.sqrt(grand_total / (total_rows * all_columns) + 1e-06)
    return (solution, scaled_residual, history, overall_rms)


def solution(mesh):
    in_specs = (P("rows", None, None), P("rows", None, None), P("rows", "rhs"))
    out_specs = (P("rows", "rhs"), P("rows", "rhs"), P(None, "rhs"), P())
    return jax.shard_map(shards, mesh=mesh, in_specs=in_specs, out_specs=out_specs, check_vma=False)
```

profile of v0, /device:TPU:1, one launch (start us, length us, event | category | flops | bytes accessed | tf_op | source)
XLA Modules:
  0.0 193.8 jit_solution(12616012140242922727)
XLA Ops:
  0.6 0.0 copy-start
  0.6 1.6 copy-done
  2.2 5.5 %fusion.314 = f32[8,256,512]{2,1,0:T(8,128)S(1)} fusion(f32[8,256,256]{2,1,0:T(8,128)S(1)} %copy-done, f32[8,256,512]{2,1,0:T(8,128)} %bitcast.289), kind=kOutput, calls=%fused_computation.183 | convolution fusion | flops 3221225472 | bytes 10485760 | tf_op jit(solution)/shard_map/jab,jbc->jac/dot_general | solution.py:50
  7.7 1.5 fusion.312
  9.2 4.5 %collective-permute-start = (f32[512,512]{1,0:T(8,128)}, f32[512,512]{1,0:T(8,128)}, u32[]{:S(2)}, u32[]{:S(2)}) collective-permute-start(f32[512,512]{1,0:T(8,128)} %bitcast.2), channel_id=1, source_target_pairs={{0,4},{4,8},{8,12},{12,16},{16,20},{20,24},{24,28},{28,32},{32,36}... | collective-permute-start | bytes 3145736 | tf_op jit(solution)/shard_map/ppermute | solution.py:14
  13.7 2.1 %collective-permute-start.1 = (f32[512,512]{1,0:T(8,128)}, f32[512,512]{1,0:T(8,128)}, u32[]{:S(2)}, u32[]{:S(2)}) collective-permute-start(f32[512,512]{1,0:T(8,128)} %bitcast.19), channel_id=1, source_target_pairs={{4,0},{8,4},{12,8},{16,12},{20,16},{24,20},{28,24},{32,28},{36,32}... | collective-permute-start | bytes 3145736 | tf_op jit(solution)/shard_map/ppermute | solution.py:17
  15.8 3.0 %fusion.313 = (f32[5,256,512]{2,1,0:T(8,128)S(1)}, f32[5,256,512]{2,1,0:T(8,128)S(1)}, f32[5,256,512]{2,1,0:T(8,128)S(1)}, f32[5,256,512]{2,1,0:T(8,128)}) fusion(f32[8,256,512]{2,1,0:T(8,128)S(1)} %fusion.314), kind=kLoop, calls=%fused_computation.182 | loop fusion | bytes 20971520 | tf_op jit(solution)/shard_map/slice | solution.py:36
  18.8 6.9 %collective-permute-done = f32[512,512]{1,0:T(8,128)} collective-permute-done((f32[512,512]{1,0:T(8,128)}, f32[512,512]{1,0:T(8,128)}, u32[]{:S(2)}, u32[]{:S(2)}) %collective-permute-start) | collective-permute-done | bytes 1048608 | tf_op jit(solution)/shard_map/ppermute | solution.py:14
  25.7 5.0 %fusion.219 = f32[2048,512]{1,0:T(8,128)} fusion(f32[512,512]{1,0:T(8,128)} %collective-permute-done, f32[2048,512]{1,0:T(8,128)S(1)} %bitcast.281, f32[8,256,1280]{2,1,0:T(8,128)} %param.3), kind=kOutput, calls=%fused_computation.129 | convolution fusion | flops 2013921280 | bytes 7077888 | tf_op jit(solution)/shard_map/dot_general | solution.py:38
  30.8 4.9 %fusion.181 = f32[2048,512]{1,0:T(8,128)} fusion(f32[2048,512]{1,0:T(8,128)} %fusion.219, f32[2048,512]{1,0:T(8,128)S(1)} %bitcast.282, f32[512,512]{1,0:T(8,128)} %collective-permute-done, f32[8,256,1280]{2,1,0:T(8,128)} %param.3), kind=kOutput, calls=%fused_computation.117 | convolution fusion | flops 2013921280 | bytes 7077888 | tf_op jit(solution)/shard_map/dot_general | solution.py:38
  35.7 4.7 %fusion.77 = f32[2048,512]{1,0:T(8,128)} fusion(f32[2048,512]{1,0:T(8,128)} %fusion.181, f32[1280,512]{1,0:T(8,128)S(1)} %bitcast.295, f32[8,256,1280]{2,1,0:T(8,128)} %param.3), kind=kOutput, calls=%fused_computation.93 | convolution fusion | flops 2013265920 | bytes 4456448 | tf_op jit(solution)/shard_map/dot_general | solution.py:38
  40.4 4.6 %fusion.83 = f32[2048,512]{1,0:T(8,128)} fusion(f32[2048,512]{1,0:T(8,128)} %fusion.77, f32[1280,512]{1,0:T(8,128)S(1)} %bitcast.294, f32[8,256,1280]{2,1,0:T(8,128)} %param.3), kind=kOutput, calls=%fused_computation.95 | convolution fusion | flops 2013265920 | bytes 4456448 | tf_op jit(solution)/shard_map/dot_general | solution.py:38
  45.0 0.0 slice-done
  45.0 3.7 %fusion.89 = f32[2048,512]{1,0:T(8,128)} fusion(f32[2048,512]{1,0:T(8,128)} %fusion.83, f32[1280,512]{1,0:T(8,128)S(1)} %bitcast.293, f32[8,256,1280]{2,1,0:T(8,128)S(1)} %bitcast.286), kind=kOutput, calls=%fused_computation.97 | convolution fusion | flops 2013265920 | bytes 4456448 | tf_op jit(solution)/shard_map/dot_general | solution.py:38
  48.7 3.3 %fusion.95 = f32[2048,512]{1,0:T(8,128)} fusion(f32[2048,512]{1,0:T(8,128)} %fusion.89, f32[1280,512]{1,0:T(8,128)S(1)} %bitcast.292, f32[8,256,1280]{2,1,0:T(8,128)S(1)} %bitcast.286), kind=kOutput, calls=%fused_computation.99 | convolution fusion | flops 2013265920 | bytes 4456448 | tf_op jit(solution)/shard_map/dot_general | solution.py:38
  52.0 0.0 collective-permute-done.1
  52.0 4.4 %fusion.229 = f32[2048,512]{1,0:T(8,128)} fusion(f32[2048,512]{1,0:T(8,128)} %fusion.95, f32[2048,512]{1,0:T(8,128)S(1)} %bitcast.283, f32[512,512]{1,0:T(8,128)} %collective-permute-done.1, f32[8,256,1280]{2,1,0:T(8,128)S(1)} %bitcast.286), kind=kOutput, calls=%fused_computation.131 | convolution fusion | flops 2013921280 | bytes 7077888 | tf_op jit(solution)/shard_map/dot_general | solution.py:38
  56.4 4.7 %fusion.187 = f32[2048,512]{1,0:T(8,128)} fusion(f32[2048,512]{1,0:T(8,128)} %fusion.229, f32[512,512]{1,0:T(8,128)} %collective-permute-done.1, f32[2048,512]{1,0:T(8,128)S(1)} %bitcast.284, f32[8,256,1280]{2,1,0:T(8,128)S(1)} %bitcast.286), kind=kOutput, calls=%fused_computation.119 | convolution fusion | flops 2013921280 | bytes 7077888 | tf_op jit(solution)/shard_map/dot_general | solution.py:38
  61.1 0.0 copy-done.2
  61.1 3.0 %multiply_reduce_fusion.2 = (f32[512]{0:T(512)S(1)}, f32[2048,512]{1,0:T(8,128)S(1)}) fusion(f32[2048,512]{1,0:T(8,128)S(1)} %copy-done.2, f32[2048,512]{1,0:T(8,128)} %fusion.187), kind=kLoop, calls=%fused_computation.16 | loop fusion | flops 3145216 | bytes 12584960 | tf_op jit(solution)/shard_map/reduce_sum | solution.py:56
  64.1 5.3 %fusion.315 = f32[8,512,256]{1,2,0:T(8,128)} fusion(f32[8,256,512]{2,1,0:T(8,128)S(1)} %bitcast.290, f32[8,256,256]{2,1,0:T(8,128)S(1)} %copy-done), kind=kOutput, calls=%fused_computation.184 | convolution fusion | flops 3221225472 | bytes 10485760 | tf_op jit(solution)/shard_map/jab,jbc->jac/dot_general | solution.py:50
  69.5 2.7 %bitcast_add_fusion.1 = f32[2048,512]{1,0:T(8,128)S(1)} fusion(f32[8,512,256]{1,2,0:T(8,128)} %fusion.315, f32[8,256,512]{2,1,0:T(8,128)S(1)} %fusion.314), kind=kLoop, calls=%fused_computation.13 | loop fusion | flops 1048576 | bytes 12582912 | tf_op jit(solution)/shard_map/add | solution.py:70
  72.2 0.2 fusion.311
  72.4 4.4 %collective-permute-start.2 = (f32[512,512]{1,0:T(8,128)S(1)}, f32[512,512]{1,0:T(8,128)S(1)}, u32[]{:S(2)}, u32[]{:S(2)}) collective-permute-start(f32[512,512]{1,0:T(8,128)S(1)} %get-tuple-element.13), channel_id=1, source_target_pairs={{0,4},{4,8},{8,12},{12,16},{16,20},{20,24},{24,28},{28,32},{32,36}... | collective-permute-start | bytes 3145736 | tf_op jit(solution)/shard_map/ppermute | solution.py:14
  76.8 2.1 %collective-permute-start.3 = (f32[512,512]{1,0:T(8,128)S(1)}, f32[512,512]{1,0:T(8,128)S(1)}, u32[]{:S(2)}, u32[]{:S(2)}) collective-permute-start(f32[512,512]{1,0:T(8,128)S(1)} %get-tuple-element.12), channel_id=1, source_target_pairs={{4,0},{8,4},{12,8},{16,12},{20,16},{24,20},{28,24},{32,28},{36,32}... | collective-permute-start | bytes 3145736 | tf_op jit(solution)/shard_map/ppermute | solution.py:17
  78.9 9.6 %collective-permute-done.2 = f32[512,512]{1,0:T(8,128)S(1)} collective-permute-done((f32[512,512]{1,0:T(8,128)S(1)}, f32[512,512]{1,0:T(8,128)S(1)}, u32[]{:S(2)}, u32[]{:S(2)}) %collective-permute-start.2) | collective-permute-done | bytes 1048608 | tf_op jit(solution)/shard_map/ppermute | solution.py:14
  88.5 2.5 %fusion.239 = f32[2048,512]{1,0:T(8,128)S(1)} fusion(f32[512,512]{1,0:T(8,128)S(1)} %collective-permute-done.2, f32[2048,512]{1,0:T(8,128)S(1)} %bitcast_add_fusion.1, f32[8,256,1280]{2,1,0:T(8,128)S(1)} %bitcast.286), kind=kOutput, calls=%fused_computation.133 | convolution fusion | flops 2013921280 | bytes 7077888 | tf_op jit(solution)/shard_map/dot_general | solution.py:38
  91.0 2.5 %fusion.193 = f32[2048,512]{1,0:T(8,128)S(1)} fusion(f32[2048,512]{1,0:T(8,128)S(1)} %fusion.239, f32[2048,512]{1,0:T(8,128)S(1)} %bitcast_add_fusion.1, f32[512,512]{1,0:T(8,128)S(1)} %collective-permute-done.2, f32[8,256,1280]{2,1,0:T(8,128)S(1)} %bitcast.286), kind=kOutput, calls=%fused_computation.121 | convolution fusion | flops 2013921280 | bytes 7077888 | tf_op jit(solution)/shard_map/dot_general | solution.py:38
  93.5 2.5 %fusion.103 = f32[2048,512]{1,0:T(8,128)S(1)} fusion(f32[2048,512]{1,0:T(8,128)S(1)} %fusion.193, f32[2048,512]{1,0:T(8,128)S(1)} %bitcast_add_fusion.1, f32[8,256,1280]{2,1,0:T(8,128)S(1)} %bitcast.286), kind=kOutput, calls=%fused_computation.101 | convolution fusion | flops 2013265920 | bytes 4456448 | tf_op jit(solution)/shard_map/dot_general | solution.py:38
  96.1 2.5 %fusion.113 = f32[2048,512]{1,0:T(8,128)S(1)} fusion(f32[2048,512]{1,0:T(8,128)S(1)} %fusion.103, f32[2048,512]{1,0:T(8,128)S(1)} %bitcast_add_fusion.1, f32[8,256,1280]{2,1,0:T(8,128)S(1)} %bitcast.286), kind=kOutput, calls=%fused_computation.103 | convolution fusion | flops 2013265920 | bytes 4456448 | tf_op jit(solution)/shard_map/dot_general | solution.py:38
  98.6 2.9 %fusion.123 = f32[2048,512]{1,0:T(8,128)S(1)} fusion(f32[2048,512]{1,0:T(8,128)S(1)} %fusion.113, f32[2048,512]{1,0:T(8,128)S(1)} %bitcast_add_fusion.1, f32[8,256,1280]{2,1,0:T(8,128)S(1)} %bitcast.286), kind=kOutput, calls=%fused_computation.105 | convolution fusion | flops 2013265920 | bytes 4456448 | tf_op jit(solution)/shard_map/dot_general | solution.py:38
  101.6 2.5 %fusion.133 = f32[2048,512]{1,0:T(8,128)S(1)} fusion(f32[2048,512]{1,0:T(8,128)S(1)} %fusion.123, f32[2048,512]{1,0:T(8,128)S(1)} %bitcast_add_fusion.1, f32[8,256,1280]{2,1,0:T(8,128)S(1)} %bitcast.286), kind=kOutput, calls=%fused_computation.107 | convolution fusion | flops 2013265920 | bytes 4456448 | tf_op jit(solution)/shard_map/dot_general | solution.py:38
  104.1 0.0 collective-permute-done.3
  104.1 2.5 %fusion.249 = f32[2048,512]{1,0:T(8,128)S(1)} fusion(f32[2048,512]{1,0:T(8,128)S(1)} %fusion.133, f32[2048,512]{1,0:T(8,128)S(1)} %bitcast_add_fusion.1, f32[512,512]{1,0:T(8,128)S(1)} %collective-permute-done.3, f32[8,256,1280]{2,1,0:T(8,128)S(1)} %bitcast.286), kind=kOutput, calls=%fused_computation.135 | convolution fusion | flops 2013921280 | bytes 7077888 | tf_op jit(solution)/shard_map/dot_general | solution.py:38
  106.6 2.5 %fusion.199 = f32[2048,512]{1,0:T(8,128)S(1)} fusion(f32[2048,512]{1,0:T(8,128)S(1)} %fusion.249, f32[512,512]{1,0:T(8,128)S(1)} %collective-permute-done.3, f32[2048,512]{1,0:T(8,128)S(1)} %bitcast_add_fusion.1, f32[8,256,1280]{2,1,0:T(8,128)S(1)} %bitcast.286), kind=kOutput, calls=%fused_computation.123 | convolution fusion | flops 2013921280 | bytes 7077888 | tf_op jit(solution)/shard_map/dot_general | solution.py:38
  109.1 0.9 multiply_reduce_fusion.1
  110.0 0.0 slice-start.4
  110.0 5.3 %fusion.316 = f32[8,512,256]{1,2,0:T(8,128)} fusion(f32[8,256,512]{2,1,0:T(8,128)S(1)} %bitcast.291, f32[8,256,256]{2,1,0:T(8,128)S(1)} %copy-done), kind=kOutput, calls=%fused_computation.185 | convolution fusion | flops 3221225472 | bytes 10485760 | tf_op jit(solution)/shard_map/jab,jbc->jac/dot_general | solution.py:50
  115.4 3.4 %bitcast_add_fusion = f32[2048,512]{1,0:T(8,128)S(1)} fusion(f32[2048,512]{1,0:T(8,128)S(1)} %bitcast_add_fusion.1, f32[8,512,256]{1,2,0:T(8,128)} %fusion.316), kind=kLoop, calls=%fused_computation.12 | loop fusion | flops 1048576 | bytes 12582912 | tf_op jit(solution)/shard_map/add | solution.py:70
  118.8 0.0 copy-start.1
  118.8 0.2 fusion.310
  118.9 4.4 %collective-permute-start.4 = (f32[512,512]{1,0:T(8,128)S(1)}, f32[512,512]{1,0:T(8,128)S(1)}, u32[]{:S(2)}, u32[]{:S(2)}) collective-permute-start(f32[512,512]{1,0:T(8,128)S(1)} %get-tuple-element.11), channel_id=1, source_target_pairs={{0,4},{4,8},{8,12},{12,16},{16,20},{20,24},{24,28},{28,32},{32,36}... | collective-permute-start | bytes 3145736 | tf_op jit(solution)/shard_map/ppermute | solution.py:14
  123.3 2.1 %collective-permute-start.5 = (f32[512,512]{1,0:T(8,128)S(1)}, f32[512,512]{1,0:T(8,128)S(1)}, u32[]{:S(2)}, u32[]{:S(2)}) collective-permute-start(f32[512,512]{1,0:T(8,128)S(1)} %get-tuple-element.10), channel_id=1, source_target_pairs={{4,0},{8,4},{12,8},{16,12},{20,16},{24,20},{28,24},{32,28},{36,32}... | collective-permute-start | bytes 3145736 | tf_op jit(solution)/shard_map/ppermute | solution.py:17
  125.4 9.6 %collective-permute-done.4 = f32[512,512]{1,0:T(8,128)S(1)} collective-permute-done((f32[512,512]{1,0:T(8,128)S(1)}, f32[512,512]{1,0:T(8,128)S(1)}, u32[]{:S(2)}, u32[]{:S(2)}) %collective-permute-start.4) | collective-permute-done | bytes 1048608 | tf_op jit(solution)/shard_map/ppermute | solution.py:14
  135.1 0.0 slice-done.5
  135.1 2.5 %fusion.259 = f32[2048,512]{1,0:T(8,128)S(1)} fusion(f32[512,512]{1,0:T(8,128)S(1)} %collective-permute-done.4, f32[2048,512]{1,0:T(8,128)S(1)} %bitcast_add_fusion, f32[8,256,1280]{2,1,0:T(8,128)S(1)} %bitcast.288), kind=kOutput, calls=%fused_computation.137 | convolution fusion | flops 2013921280 | bytes 7077888 | tf_op jit(solution)/shard_map/dot_general | solution.py:38
  137.6 2.5 %fusion.205 = f32[2048,512]{1,0:T(8,128)S(1)} fusion(f32[2048,512]{1,0:T(8,128)S(1)} %fusion.259, f32[2048,512]{1,0:T(8,128)S(1)} %bitcast_add_fusion, f32[512,512]{1,0:T(8,128)S(1)} %collective-permute-done.4, f32[8,256,1280]{2,1,0:T(8,128)S(1)} %bitcast.288), kind=kOutput, calls=%fused_computation.125 | convolution fusion | flops 2013921280 | bytes 7077888 | tf_op jit(solution)/shard_map/dot_general | solution.py:38
  140.1 2.5 %fusion.143 = f32[2048,512]{1,0:T(8,128)S(1)} fusion(f32[2048,512]{1,0:T(8,128)S(1)} %fusion.205, f32[2048,512]{1,0:T(8,128)S(1)} %bitcast_add_fusion, f32[8,256,1280]{2,1,0:T(8,128)S(1)} %bitcast.288), kind=kOutput, calls=%fused_computation.109 | convolution fusion | flops 2013265920 | bytes 4456448 | tf_op jit(solution)/shard_map/dot_general | solution.py:38
  142.6 2.5 %fusion.153 = f32[2048,512]{1,0:T(8,128)S(1)} fusion(f32[2048,512]{1,0:T(8,128)S(1)} %fusion.143, f32[2048,512]{1,0:T(8,128)S(1)} %bitcast_add_fusion, f32[8,256,1280]{2,1,0:T(8,128)S(1)} %bitcast.288), kind=kOutput, calls=%fused_computation.111 | convolution fusion | flops 2013265920 | bytes 4456448 | tf_op jit(solution)/shard_map/dot_general | solution.py:38
  145.1 2.7 %fusion.163 = f32[2048,512]{1,0:T(8,128)S(1)} fusion(f32[2048,512]{1,0:T(8,128)S(1)} %fusion.153, f32[2048,512]{1,0:T(8,128)S(1)} %bitcast_add_fusion, f32[8,256,1280]{2,1,0:T(8,128)S(1)} %bitcast.288), kind=kOutput, calls=%fused_computation.113 | convolution fusion | flops 2013265920 | bytes 4456448 | tf_op jit(solution)/shard_map/dot_general | solution.py:38
  147.9 2.5 %fusion.173 = f32[2048,512]{1,0:T(8,128)S(1)} fusion(f32[2048,512]{1,0:T(8,128)S(1)} %fusion.163, f32[2048,512]{1,0:T(8,128)S(1)} %bitcast_add_fusion, f32[8,256,1280]{2,1,0:T(8,128)S(1)} %bitcast.288), kind=kOutput, calls=%fused_computation.115 | convolution fusion | flops 2013265920 | bytes 4456448 | tf_op jit(solution)/shard_map/dot_general | solution.py:38
  150.4 0.0 collective-permute-done.5
  150.4 2.5 %fusion.269 = f32[2048,512]{1,0:T(8,128)S(1)} fusion(f32[2048,512]{1,0:T(8,128)S(1)} %fusion.173, f32[2048,512]{1,0:T(8,128)S(1)} %bitcast_add_fusion, f32[512,512]{1,0:T(8,128)S(1)} %collective-permute-done.5, f32[8,256,1280]{2,1,0:T(8,128)S(1)} %bitcast.288), kind=kOutput, calls=%fused_computation.139 | convolution fusion | flops 2013921280 | bytes 7077888 | tf_op jit(solution)/shard_map/dot_general | solution.py:38
  152.9 2.5 %fusion.211 = f32[2048,512]{1,0:T(8,128)S(1)} fusion(f32[2048,512]{1,0:T(8,128)S(1)} %fusion.269, f32[512,512]{1,0:T(8,128)S(1)} %collective-permute-done.5, f32[2048,512]{1,0:T(8,128)S(1)} %bitcast_add_fusion, f32[8,256,1280]{2,1,0:T(8,128)S(1)} %bitcast.288), kind=kOutput, calls=%fused_computation.127 | convolution fusion | flops 2013921280 | bytes 7077888 | tf_op jit(solution)/shard_map/dot_general | solution.py:38
  155.4 2.9 %multiply_reduce_fusion = (f32[512]{0:T(512)S(1)}, f32[2048,512]{1,0:T(8,128)}) fusion(f32[2048,512]{1,0:T(8,128)S(1)} %copy-done.2, f32[2048,512]{1,0:T(8,128)S(1)} %fusion.211), kind=kLoop, calls=%fused_computation.14 | loop fusion | flops 3145216 | bytes 12584960 | tf_op jit(solution)/shard_map/reduce_sum | solution.py:56
  158.4 21.0 %all_to_all.11 = f32[32,3,512]{2,1,0:T(4,128)S(1)} all-to-all(f32[32,3,512]{2,1,0:T(4,128)S(1)} %broadcast_in_dim.6), channel_id=1, replica_groups=mesh['rows'=32,'rhs'=4] {'rows'}, dimensions={0} | all-to-all | bytes 393216 | tf_op jit(solution)/shard_map/all_to_all | solution.py:24
  179.5 0.1 reduce_sum.57
  179.5 0.6 slice_reduce_fusion
  180.1 0.0 copy-start.4
  180.2 1.2 broadcast_in_dim.7
  181.4 5.0 %all-to-all-start.1 = ((f32[4,1,1]{2,1,0:T(1,128)}), f32[4,1,1]{2,1,0:T(1,128)S(1)}, u32[]{:S(2)}, u32[]{:S(2)}) async-start(f32[4,1,1]{2,1,0:T(1,128)} %broadcast_in_dim.7), calls=%async_computation.1 | async-start | bytes 4096 | tf_op jit(solution)/shard_map/all_to_all | solution.py:24
  186.4 4.7 %broadcast_divide_fusion = f32[2048,512]{1,0:T(8,128)} fusion(f32[2048,512]{1,0:T(8,128)} %get-tuple-element.9, f32[512]{0:T(512)S(1)} %bitcast.296), kind=kLoop, calls=%fused_computation.63 | loop fusion | flops 1048576 | bytes 8390656 | tf_op jit(solution)/shard_map/div | solution.py:76
  191.2 0.0 all-to-all-done.1
  191.2 0.6 reduce_sum.59
  (20 shorter events, 0.1 us)
Async XLA Ops:
  0.6 1.6 copy-start
  9.2 16.5 %collective-permute-start = (f32[512,512]{1,0:T(8,128)}, f32[512,512]{1,0:T(8,128)}, u32[]{:S(2)}, u32[]{:S(2)}) collective-permute-start(f32[512,512]{1,0:T(8,128)} %bitcast.2), channel_id=1, source_target_pairs={{0,4},{4,8},{8,12},{12,16},{16,20},{20,24},{24,28},{28,32},{32,36}... | collective-permute-start | bytes 3145736 | tf_op jit(solution)/shard_map/ppermute | solution.py:14
  13.7 38.3 %collective-permute-start.1 = (f32[512,512]{1,0:T(8,128)}, f32[512,512]{1,0:T(8,128)}, u32[]{:S(2)}, u32[]{:S(2)}) collective-permute-start(f32[512,512]{1,0:T(8,128)} %bitcast.19), channel_id=1, source_target_pairs={{4,0},{8,4},{12,8},{16,12},{20,16},{24,20},{28,24},{32,28},{36,32}... | collective-permute-start | bytes 3145736 | tf_op jit(solution)/shard_map/ppermute | solution.py:17
  25.7 19.2 %slice-start = ((s8[10485760]{0:T(1024)(128)(4,1)}), s8[4194304]{0:T(1024)(128)(4,1)S(1)}, s32[]{:S(2)}) async-start(s8[10485760]{0:T(1024)(128)(4,1)} %bitcast.285), calls=%async_computation.2 | async-start | bytes 8388608
  30.8 4.9 %copy-start.3 = (f32[5,256,512]{2,1,0:T(8,128)S(1)}, f32[5,256,512]{2,1,0:T(8,128)}, u32[]{:S(2)}) copy-start(f32[5,256,512]{2,1,0:T(8,128)} %get-tuple-element.19) | copy-start | bytes 7864324
  30.8 14.2 %slice-start.1 = ((s8[10485760]{0:T(1024)(128)(4,1)}), s8[4194304]{0:T(1024)(128)(4,1)S(1)}, s32[]{:S(2)}) async-start(s8[10485760]{0:T(1024)(128)(4,1)} %bitcast.285), calls=%async_computation.3 | async-start | bytes 8388608
  35.7 9.3 %slice-start.2 = ((s8[10485760]{0:T(1024)(128)(4,1)}), s8[2097152]{0:T(1024)(128)(4,1)S(1)}, s32[]{:S(2)}) async-start(s8[10485760]{0:T(1024)(128)(4,1)} %bitcast.285), calls=%async_computation.4 | async-start | bytes 4194304
  56.4 4.7 %copy-start.2 = (f32[2048,512]{1,0:T(8,128)S(1)}, f32[2048,512]{1,0:T(8,128)}, u32[]{:S(2)}) copy-start(f32[2048,512]{1,0:T(8,128)} %param.5) | copy-start | bytes 12582916
  72.4 16.1 %collective-permute-start.2 = (f32[512,512]{1,0:T(8,128)S(1)}, f32[512,512]{1,0:T(8,128)S(1)}, u32[]{:S(2)}, u32[]{:S(2)}) collective-permute-start(f32[512,512]{1,0:T(8,128)S(1)} %get-tuple-element.13), channel_id=1, source_target_pairs={{0,4},{4,8},{8,12},{12,16},{16,20},{20,24},{24,28},{28,32},{32,36}... | collective-permute-start | bytes 3145736 | tf_op jit(solution)/shard_map/ppermute | solution.py:14
  76.8 27.3 %collective-permute-start.3 = (f32[512,512]{1,0:T(8,128)S(1)}, f32[512,512]{1,0:T(8,128)S(1)}, u32[]{:S(2)}, u32[]{:S(2)}) collective-permute-start(f32[512,512]{1,0:T(8,128)S(1)} %get-tuple-element.12), channel_id=1, source_target_pairs={{4,0},{8,4},{12,8},{16,12},{20,16},{24,20},{28,24},{32,28},{36,32}... | collective-permute-start | bytes 3145736 | tf_op jit(solution)/shard_map/ppermute | solution.py:17
  110.0 25.0 %slice-start.3 = ((s8[10485760]{0:T(1024)(128)(4,1)}), s8[4194304]{0:T(1024)(128)(4,1)S(1)}, s32[]{:S(2)}) async-start(s8[10485760]{0:T(1024)(128)(4,1)} %bitcast.287), calls=%async_computation.5 | async-start | bytes 8388608
  110.0 25.0 %slice-start.4 = ((s8[10485760]{0:T(1024)(128)(4,1)}), s8[4194304]{0:T(1024)(128)(4,1)S(1)}, s32[]{:S(2)}) async-start(s8[10485760]{0:T(1024)(128)(4,1)} %bitcast.287), calls=%async_computation.6 | async-start | bytes 8388608
  115.4 19.7 %slice-start.5 = ((s8[10485760]{0:T(1024)(128)(4,1)}), s8[2097152]{0:T(1024)(128)(4,1)S(1)}, s32[]{:S(2)}) async-start(s8[10485760]{0:T(1024)(128)(4,1)} %bitcast.287), calls=%async_computation.7 | async-start | bytes 4194304
  118.8 34.2 %copy-start.1 = (f32[2048,512]{1,0:T(8,128)}, f32[2048,512]{1,0:T(8,128)S(1)}, u32[]{:S(2)}) copy-start(f32[2048,512]{1,0:T(8,128)S(1)} %bitcast_add_fusion) | copy-start | bytes 12582916
  118.9 16.1 %collective-permute-start.4 = (f32[512,512]{1,0:T(8,128)S(1)}, f32[512,512]{1,0:T(8,128)S(1)}, u32[]{:S(2)}, u32[]{:S(2)}) collective-permute-start(f32[512,512]{1,0:T(8,128)S(1)} %get-tuple-element.11), channel_id=1, source_target_pairs={{0,4},{4,8},{8,12},{12,16},{16,20},{20,24},{24,28},{28,32},{32,36}... | collective-permute-start | bytes 3145736 | tf_op jit(solution)/shard_map/ppermute | solution.py:14
  123.3 27.0 %collective-permute-start.5 = (f32[512,512]{1,0:T(8,128)S(1)}, f32[512,512]{1,0:T(8,128)S(1)}, u32[]{:S(2)}, u32[]{:S(2)}) collective-permute-start(f32[512,512]{1,0:T(8,128)S(1)} %get-tuple-element.10), channel_id=1, source_target_pairs={{4,0},{8,4},{12,8},{16,12},{20,16},{24,20},{28,24},{32,28},{36,32}... | collective-permute-start | bytes 3145736 | tf_op jit(solution)/shard_map/ppermute | solution.py:17
  180.1 11.0 %copy-start.4 = (f32[3,512]{1,0:T(4,128)}, f32[3,512]{1,0:T(4,128)S(1)}, u32[]{:S(2)}) copy-start(f32[3,512]{1,0:T(4,128)S(1)} %add_sqrt_fusion) | copy-start | bytes 18436
  181.4 9.8 %all-to-all-start.1 = ((f32[4,1,1]{2,1,0:T(1,128)}), f32[4,1,1]{2,1,0:T(1,128)S(1)}, u32[]{:S(2)}, u32[]{:S(2)}) async-start(f32[4,1,1]{2,1,0:T(1,128)} %broadcast_in_dim.7), calls=%async_computation.1 | async-start | bytes 4096 | tf_op jit(solution)/shard_map/all_to_all | solution.py:24
where the time goes:
time: 197 us; the launch traced here: 194 us
  matrix products  92.3 us (47%)
  waiting for transfers between devices  26.1 us (13%)
  starting transfers between devices  24.6 us (12%)
  blocking collectives  21 us (11%)
  other arithmetic  19 us (10%)
  local copies, waits for them, and re-layouts  7.76 us (4%)
  between operations  3 us (2%)
    dot_general x24, matrix products, band_times(): jnp.dot(band_blocks[number], window, precision=lax.Precision.HIGHEST, pre...  76.2 us
    ppermute x3, waiting for transfers between devices, extended(): lax.ppermute(lax.slice_in_dim(block, block.shape[dim] - width, None, axis...  26.1 us
    all_to_all x1, blocking collectives, sent_to_all(): return lax.all_to_all(copies, axis, split_axis=0, concat_axis=0, tiled=True)  21 us
    dot_general x3, matrix products, precondition(): jnp.einsum('jab,jbc->jac', precond_blocks, shaped, precision=lax.Precisio...  16.2 us
    ppermute x3, starting transfers between devices, extended(): lax.ppermute(lax.slice_in_dim(block, block.shape[dim] - width, None, axis...  13.3 us
    reduce_sum x3, other arithmetic, column_squares(): partial_value = jnp.sum(residual * residual, axis=0)  6.86 us
    ppermute x3, starting transfers between devices, extended(): lax.ppermute(lax.slice_in_dim(block, 0, width, axis=dim), axis, backward)  6.29 us
    add x2, other arithmetic, shards(): solution = solution + precondition(precond_blocks, residual)  6.08 us
  transfers between devices with their start and end apart: 7, of which 3 were waited for; matrix products, arithmetic and copies ran while one was open for 33% of the time, Pallas kernels for 0%

commit v1 on v0

v1 whole, which is shorter than its diff:
```python
import functools

import jax
import jax.numpy as jnp
from jax import lax
from jax.experimental import pallas as pl
from jax.experimental.pallas import tpu as pltpu
from jax.sharding import PartitionSpec as P

MESH = pl.DeviceIdType.MESH
F32, BF16 = jnp.float32, jnp.bfloat16
SWEEPS = 3
T = 256
LINE = 8


def split(value):
    high = value.astype(BF16)
    return high, (value - high.astype(F32)).astype(BF16)


def kernel(
    rows_n, rhs_n, blocks,
    band, precond, rhs,
    x, r, history, overall,
    a32, m32, ahi, alo, mhi, mlo, rhi, rlo, dhi, dlo, dsend, halo, hhi, hlo, part, msg, p1, mid, p2, zmsg, zbuf,
    a_sem, m_sem, b_sem, send_sem, recv_sem, p1_send, p1_recv, p2_send, p2_recv, z_send, z_recv,
):
    me = lax.axis_index("rows")
    z = lax.axis_index("rhs")
    lines = rows_n // LINE
    line, spot = me // LINE, me % LINE
    has = (me > 0, me < rows_n - 1)
    beside = (me - 1, me + 1)
    far = ((spot == 0) & has[0], (spot == LINE - 1) & has[1])
    chunks = rhs.shape[1] // T
    edge = (0, 1, blocks - 1, blocks - 2)
    inner = tuple(range(2, blocks // 2)), tuple(range(blocks - 3, blocks // 2 - 1, -1))
    inner_flat = tuple(j for pair in zip(*inner) for j in pair)

    def rows_of(j):
        return slice(j * T, (j + 1) * T)

    def cols_of(c):
        if isinstance(c, int):
            return slice(c * T, (c + 1) * T)
        return pl.ds(pl.multiple_of(c * T, T), T)

    def m_copy(j):
        return pltpu.make_async_copy(precond.at[j], m32.at[j], m_sem.at[j])

    def b_copy(j, c):
        return pltpu.make_async_copy(
            rhs.at[rows_of(j), cols_of(c)], r.at[rows_of(j), cols_of(c)], b_sem.at[j, c]
        )

    def a_copy(j):
        return pltpu.make_async_copy(band.at[j], a32.at[j], a_sem.at[j])

    for j in edge:
        m_copy(j).start()
    for c in range(chunks):
        for j in edge:
            b_copy(j, c).start()
    for j in inner_flat:
        m_copy(j).start()
    for c in range(chunks):
        for j in inner_flat:
            b_copy(j, c).start()
    for j in (*edge, *inner_flat):
        a_copy(j).start()

    barrier = pltpu.get_barrier_semaphore()
    for k in range(1, LINE):
        pl.semaphore_signal(
            barrier, inc=1, device_id={"rows": line * LINE + (spot + k) % LINE}, device_id_type=MESH
        )
    for k in range(1, lines):
        pl.semaphore_signal(
            barrier, inc=1, device_id={"rows": (line + k) % lines * LINE + spot}, device_id_type=MESH
        )
    for k in range(1, rhs_n):
        pl.semaphore_signal(barrier, inc=1, device_id={"rhs": (z + k) % rhs_n}, device_id_type=MESH)
    for side in range(2):

        @pl.when(far[side])
        def _():
            pl.semaphore_signal(barrier, inc=1, device_id={"rows": beside[side]}, device_id_type=MESH)

    peers = LINE - 1 + lines - 1 + rhs_n - 1

    part[...] = jnp.zeros_like(part)
    for side in range(2):

        @pl.when(jnp.logical_not(has[side]))
        def _():
            halo[:, :, side] = jnp.zeros_like(halo[:, :, side])

    def body(*accs):
        acc = (accs[:2], accs[2:])
        turn = [0]

        def products(jobs):
            pick = turn[0] % 2
            turn[0] += 1
            for step in range(max(len(job) for job in jobs)):
                for unit in range(2):
                    if step < len(jobs[unit]):
                        pltpu.matmul_push_rhs(
                            jobs[unit][step][0][...], staging_register=step % 2, mxu_index=unit
                        )
                for unit in range(2):
                    if step < len(jobs[unit]):
                        staged = step % 2
                        for left in jobs[unit][step][1]:
                            pltpu.matmul_acc_lhs(acc[unit][pick], left[...], load_staged_rhs=staged)
                            staged = None
            return [pltpu.matmul_pop(acc[unit][pick]) for unit in range(2)]

        def terms(left_high, left_low, right_high, right_low):
            return [(right_high, (left_high, left_low)), (right_low, (left_high,))]

        def band_terms(i, k, right_high, right_low):
            cut = (i, slice(None), slice(k * T, (k + 1) * T))
            return terms(ahi.at[cut], alo.at[cut], right_high, right_low)

        def precondition(pairs, c, first):
            for pair in pairs:
                values = products(
                    [terms(mhi.at[j], mlo.at[j], rhi.at[c, j], rlo.at[c, j]) for j in pair]
                )
                for j, value in zip(pair, values):
                    where = (rows_of(j), cols_of(c))
                    if first:
                        x[where] = value
                    else:
                        x[where] = x[where] + value
                    dhi[c, j], dlo[c, j] = split(value)
                    if j < 2:
                        dsend[c, 0, j] = value
                    elif j >= blocks - 2:
                        dsend[c, 1, j - (blocks - 2)] = value

        def settle(s, c, j, value, keep):
            where = (rows_of(j), cols_of(c))
            value = r[where] - value
            r[where] = value
            if keep:
                rhi[c, j], rlo[c, j] = split(value)
            return value

        def squares(s, c, values):
            total = part[s, c]
            for value in values:
                total = total + jnp.sum((value * value).reshape(T // 8, 8, T), axis=0)
            part[s, c] = total

        def local(s, c):
            for pair in zip(*((0, 1, *inner[0]), (blocks - 1, blocks - 2, *inner[1]))):
                jobs = []
                for i in pair:
                    job = []
                    for k in range(5):
                        j = i + k - 2
                        if 0 <= j < blocks:
                            job += band_terms(i, k, dhi.at[c, j], dlo.at[c, j])
                    jobs.append(job)
                values = products(jobs)
                for i, value in zip(pair, values):
                    if i in edge:
                        where = (rows_of(i), cols_of(c))
                        r[where] = r[where] - value
                    else:
                        squares(s, c, [settle(s, c, i, value, True)])

        def halo_copy(s, c, side):
            return pltpu.make_async_remote_copy(
                src_ref=dsend.at[c, side],
                dst_ref=halo.at[s, c, 1 - side],
                send_sem=send_sem.at[s, c, side],
                recv_sem=recv_sem.at[s, c, 1 - side],
                device_id={"rows": beside[side]},
                device_id_type=MESH,
            )

        def send(s, c):
            for side in range(2):

                @pl.when(has[side])
                def _():
                    halo_copy(s, c, side).start()

        def sent(s, c):
            for side in range(2):

                @pl.when(has[side])
                def _():
                    halo_copy(s, c, side).wait_send()

        def remote(s, c, keep):
            for side in range(2):

                @pl.when(has[side])
                def _():
                    pltpu.make_async_remote_copy(
                        src_ref=dsend.at[c, side],
                        dst_ref=halo.at[s, c, side],
                        send_sem=send_sem.at[s, c, side],
                        recv_sem=recv_sem.at[s, c, side],
                        device_id={"rows": beside[side]},
                        device_id_type=MESH,
                    ).wait_recv()

            for side in range(2):
                for q in range(2):
                    hhi[side, q], hlo[side, q] = split(halo[s, c, side, q])
            low = lambda q: (hhi.at[0, q], hlo.at[0, q])
            high = lambda q: (hhi.at[1, q], hlo.at[1, q])
            for pair, jobs in (
                (
                    (0, blocks - 1),
                    (
                        band_terms(0, 0, *low(0)) + band_terms(0, 1, *low(1)),
                        band_terms(blocks - 1, 3, *high(0)) + band_terms(blocks - 1, 4, *high(1)),
                    ),
                ),
                (
                    (1, blocks - 2),
                    (band_terms(1, 0, *low(1)), band_terms(blocks - 2, 4, *high(0))),
                ),
            ):
                values = products(jobs)
                squares(s, c, [settle(s, c, i, value, keep) for i, value in zip(pair, values)])

        def p1_copy(s, c, k):
            return pltpu.make_async_remote_copy(
                src_ref=msg.at[s, c],
                dst_ref=p1.at[s, c, k],
                send_sem=p1_send.at[s, c, k],
                recv_sem=p1_recv.at[s, c, k],
                device_id={"rows": line * LINE + (spot + k) % LINE},
                device_id_type=MESH,
            )

        def p2_copy(s, c, k):
            return pltpu.make_async_remote_copy(
                src_ref=mid.at[s, c],
                dst_ref=p2.at[s, c, k],
                send_sem=p2_send.at[s, c, k],
                recv_sem=p2_recv.at[s, c, k],
                device_id={"rows": (line + k) % lines * LINE + spot},
                device_id_type=MESH,
            )

        def sum_line(s, c):
            msg[s, c] = jnp.sum(part[s, c], axis=0, keepdims=True)
            for k in range(1, LINE):
                p1_copy(s, c, k).start()

        def sum_lines(s, c):
            total = msg[s, c]
            for k in range(1, LINE):
                p1_copy(s, c, k).wait()
                total = total + p1[s, c, k]
            mid[s, c] = total
            for k in range(1, lines):
                p2_copy(s, c, k).start()

        def summed(s, c):
            total = mid[s, c]
            for k in range(1, lines):
                p2_copy(s, c, k).wait()
                total = total + p2[s, c, k]
            return total

        def ready_rhs(js, c):
            for j in js:
                b_copy(j, c).wait()
                rhi[c, j], rlo[c, j] = split(r[rows_of(j), cols_of(c)])

        def ready_precond(js):
            for j in js:
                m_copy(j).wait()
                mhi[j], mlo[j] = split(m32[j])

        edge_pairs = ((0, blocks - 1), (1, blocks - 2))
        inner_pairs = tuple(zip(*inner))

        ready_precond(edge)
        for c in range(chunks):
            ready_rhs(edge, c)
            precondition(edge_pairs, c, True)
            if c == 0:
                pl.semaphore_wait(
                    barrier, peers + far[0].astype(jnp.int32) + far[1].astype(jnp.int32)
                )
            send(0, c)
        ready_precond(inner_flat)
        for c in range(chunks):
            ready_rhs(inner_flat, c)
            precondition(inner_pairs, c, True)
        for j in (*edge, *inner_flat):
            a_copy(j).wait()
            ahi[j], alo[j] = split(a32[j])

        def first_local(c, carry):
            local(0, c)
            return carry

        lax.fori_loop(0, chunks, first_local, 0)

        def unit(u, carry):
            s, c = u // chunks, u % chunks
            remote(s, c, True)
            sent(s, c)
            precondition(edge_pairs, c, False)
            send(s + 1, c)
            sum_line(s, c)
            precondition(inner_pairs, c, False)
            local(s + 1, c)
            sum_lines(s, c)
            return carry

        lax.fori_loop(0, (SWEEPS - 1) * chunks, unit, 0)

        last = SWEEPS - 1
        for c in range(chunks):
            remote(last, c, False)
            sum_line(last, c)
            sent(last, c)
            if c > 0:
                sum_lines(last, c - 1)
        sum_lines(last, chunks - 1)
        for s in range(SWEEPS - 1):
            for c in range(chunks):
                history[s : s + 1, cols_of(c)] = jnp.sqrt(
                    summed(s, c) / (rows_n * blocks * T) + 1e-06
                )
        grand = jnp.zeros((1, 1), F32)
        roots = []
        for c in range(chunks):
            total = summed(last, c)
            grand = grand + jnp.sum(total, axis=1, keepdims=True)
            root = jnp.sqrt(total / (rows_n * blocks * T) + 1e-06)
            history[last : last + 1, cols_of(c)] = root
            roots.append(root)
        zmsg[...] = jnp.broadcast_to(grand, zmsg.shape)

        def z_copy(k):
            return pltpu.make_async_remote_copy(
                src_ref=zmsg,
                dst_ref=zbuf.at[k],
                send_sem=z_send.at[k],
                recv_sem=z_recv.at[k],
                device_id={"rhs": (z + k) % rhs_n},
                device_id_type=MESH,
            )

        for k in range(1, rhs_n):
            z_copy(k).start()
        for c in range(chunks):
            inverse = 1.0 / roots[c]
            for j in range(blocks):
                where = (rows_of(j), cols_of(c))
                r[where] = r[where] * inverse
        grand = zmsg[...]
        for k in range(1, rhs_n):
            z_copy(k).wait()
            grand = grand + zbuf[k]
        overall[...] = jnp.sqrt(grand / (rows_n * blocks * T * rhs_n * rhs.shape[1]) + 1e-06)

    pl.run_scoped(body, *([pltpu.ACC(0)((T, T), F32)] * 2), *([pltpu.ACC(1)((T, T), F32)] * 2))


def shards(rows_n, rhs_n, band_blocks, precond_blocks, right_side):
    blocks = band_blocks.shape[0]
    n_rows, n_cols = right_side.shape
    chunks = n_cols // T
    band_blocks, precond_blocks, right_side = (
        pltpu.with_memory_space_constraint(v, pltpu.HBM) for v in (band_blocks, precond_blocks, right_side)
    )
    dma = pltpu.SemaphoreType.DMA
    vmem = pltpu.VMEM
    x, r, history, overall = pl.pallas_call(
        functools.partial(kernel, rows_n, rhs_n, blocks),
        out_shape=(
            vmem((n_rows, n_cols), F32),
            vmem((n_rows, n_cols), F32),
            jax.ShapeDtypeStruct((SWEEPS, n_cols), F32),
            jax.ShapeDtypeStruct((1, 128), F32),
        ),
        in_specs=[pl.BlockSpec(memory_space=pltpu.HBM)] * 3,
        out_specs=[pl.BlockSpec(memory_space=vmem)] * 4,
        scratch_shapes=[
            vmem((blocks, T, 5 * T), F32),
            vmem((blocks, T, T), F32),
            vmem((blocks, T, 5 * T), BF16),
            vmem((blocks, T, 5 * T), BF16),
            vmem((blocks, T, T), BF16),
            vmem((blocks, T, T), BF16),
            vmem((chunks, blocks, T, T), BF16),
            vmem((chunks, blocks, T, T), BF16),
            vmem((chunks, blocks, T, T), BF16),
            vmem((chunks, blocks, T, T), BF16),
            vmem((chunks, 2, 2, T, T), F32),
            vmem((SWEEPS, chunks, 2, 2, T, T), F32),
            vmem((2, 2, T, T), BF16),
            vmem((2, 2, T, T), BF16),
            vmem((SWEEPS, chunks, 8, T), F32),
            vmem((SWEEPS, chunks, 1, T), F32),
            vmem((SWEEPS, chunks, LINE, 1, T), F32),
            vmem((SWEEPS, chunks, 1, T), F32),
            vmem((SWEEPS, chunks, rows_n // LINE, 1, T), F32),
            vmem((1, 128), F32),
            vmem((rhs_n, 1, 128), F32),
            dma((blocks,)),
            dma((blocks,)),
            dma((blocks, chunks)),
            dma((SWEEPS, chunks, 2)),
            dma((SWEEPS, chunks, 2)),
            dma((SWEEPS, chunks, LINE)),
            dma((SWEEPS, chunks, LINE)),
            dma((SWEEPS, chunks, rows_n // LINE)),
            dma((SWEEPS, chunks, rows_n // LINE)),
            dma((rhs_n,)),
            dma((rhs_n,)),
        ],
        compiler_params=pltpu.CompilerParams(
            collective_id=0, has_side_effects=True, vmem_limit_bytes=50 * 1024 * 1024
        ),
        name="refine",
    )(band_blocks, precond_blocks, right_side)
    return x, r, history, overall[0, 0]


def solution(mesh):
    rows_n, rhs_n = mesh.shape["rows"], mesh.shape["rhs"]
    in_specs = (P("rows", None, None), P("rows", None, None), P("rows", "rhs"))
    out_specs = (P("rows", "rhs"), P("rows", "rhs"), P(None, "rhs"), P())
    return jax.shard_map(
        functools.partial(shards, rows_n, rhs_n),
        mesh=mesh,
        in_specs=in_specs,
        out_specs=out_specs,
        check_vma=False,
    )
```

time: 197 us -> 83.3 us (0.42); the launches traced: 194 us -> 82.4 us
  matrix products: 92.3 us -> 0 us
  Pallas kernels: 0 us -> 76 us
  waiting for transfers between devices: 26.1 us -> 0 us
  starting transfers between devices: 24.6 us -> 0 us
  blocking collectives: 21 us -> 0 us
  other arithmetic: 19 us -> 0 us
  local copies, waits for them, and re-layouts: 7.76 us -> 4.63 us
    dot_general x27 -> x0, matrix products: 92.3 us -> none  [the longest x24 76.2 us: band_times(): jnp.dot(band_blocks[number], window, precision=lax.Precision.HIGHEST, pre...]
    pallas_call x0 -> x1, Pallas kernels: none -> 76 us  [shards(): pl.pallas_call(functools.partial(kernel, rows_n, rhs_n, blocks), out_shap...]
    ppermute x6 -> x0, waiting for transfers between devices: 26.1 us -> none  [the longest x3 26.1 us: extended(): lax.ppermute(lax.slice_in_dim(block, block.shape[dim] - width, None, axis...]
    all_to_all x1 -> x0, blocking collectives: 21 us -> none  [sent_to_all(): return lax.all_to_all(copies, axis, split_axis=0, concat_axis=0, tiled=True)]
    ppermute x6 -> x0, starting transfers between devices: 19.6 us -> none  [the longest x3 13.3 us: extended(): lax.ppermute(lax.slice_in_dim(block, block.shape[dim] - width, None, axis...]
    reduce_sum x6 -> x0, other arithmetic: 8.13 us -> none  [the longest x3 6.86 us: column_squares(): partial_value = jnp.sum(residual * residual, axis=0)]
    add x2 -> x0, other arithmetic: 6.08 us -> none  [shards(): solution = solution + precondition(precond_blocks, residual)]
    all_to_all x1 -> x0, starting transfers between devices: 5.02 us -> none  [sent_to_all(): return lax.all_to_all(copies, axis, split_axis=0, concat_axis=0, tiled=True)]
  transfers between devices with their start and end apart: 7 -> 0, of which waited for: 3 -> 0; matrix products, arithmetic and copies ran while one was open for 33% -> 0% of each run, Pallas kernels for 0% -> 0%
where the time goes in v1:
time: 83.3 us; the launch traced here: 82.4 us
  Pallas kernels  76 us (91%)
  local copies, waits for them, and re-layouts  4.63 us (6%)
  between operations  1.81 us (2%)
    pallas_call x1, Pallas kernels, shards(): pl.pallas_call(functools.partial(kernel, rows_n, rhs_n, blocks), out_shap...  76 us
    unnamed x7, local copies, waits for them, and re-layouts  4.63 us

profile of v1, /device:TPU:1, one launch (start us, length us, event | category | flops | bytes accessed | tf_op | source)
XLA Modules:
  0.0 82.4 jit_solution(5455272525519855114)
XLA Ops:
  0.6 76.0 %refine.1 = (f32[2048,512]{1,0:T(8,128)S(1)}, f32[2048,512]{1,0:T(8,128)S(1)}, f32[3,512]{1,0:T(4,128)}, f32[1,128]{1,0:T(1,128)}) custom-call(f32[8,256,1280]{2,1,0:T(8,128)} %band.1, f32[8,256,256]{2,1,0:T(8,128)} %precond.1, f32[2048,512]{1,0:T(8,128)} %rhs.1), custom_call_target="tpu_custom_call" | custom-call | tf_op jit(solution)/shard_map/refine/pallas_call | solution.py:384
  76.6 2.0 %copy.11 = f32[2048,512]{1,0:T(8,128)} copy(f32[2048,512]{1,0:T(8,128)S(1)} %get-tuple-element.12) | data formatting | bytes 8388608
  78.6 0.0 copy-start
  78.6 0.0 copy-start.1
  78.6 2.0 %copy.12 = f32[2048,512]{1,0:T(8,128)} copy(f32[2048,512]{1,0:T(8,128)S(1)} %get-tuple-element.13) | data formatting | bytes 8388608
  80.7 0.0 copy-done
  80.7 0.6 copy.13
  81.3 0.0 copy-done.1
Async XLA Ops:
  78.6 2.0 %copy-start = (f32[3,512]{1,0:T(4,128)S(1)}, f32[3,512]{1,0:T(4,128)}, u32[]{:S(2)}) copy-start(f32[3,512]{1,0:T(4,128)} %get-tuple-element.22) | copy-start | bytes 18436
  78.6 2.6 %copy-start.1 = (f32[1,128]{1,0:T(1,128)S(1)}, f32[1,128]{1,0:T(1,128)}, u32[]{:S(2)}) copy-start(f32[1,128]{1,0:T(1,128)} %get-tuple-element.11) | copy-start | bytes 1540

commit v2 on v1

--- a/solution.py
+++ b/solution.py
@@ -11,6 +11,7 @@
 F32, BF16 = jnp.float32, jnp.bfloat16
 SWEEPS = 3
 T = 256
+PIECES = 4
 LINE = 8
 
 
@@ -67,8 +68,10 @@
     for c in range(chunks):
         for j in inner_flat:
             b_copy(j, c).start()
-    for j in (*edge, *inner_flat):
-        a_copy(j).start()
+    band_pairs = tuple(zip((0, 1, *inner[0]), (blocks - 1, blocks - 2, *inner[1])))
+    for pair in band_pairs:
+        for j in pair:
+            a_copy(j).start()
 
     barrier = pltpu.get_barrier_semaphore()
     for k in range(1, LINE):
@@ -88,13 +91,6 @@
             pl.semaphore_signal(barrier, inc=1, device_id={"rows": beside[side]}, device_id_type=MESH)
 
     peers = LINE - 1 + lines - 1 + rhs_n - 1
-
-    part[...] = jnp.zeros_like(part)
-    for side in range(2):
-
-        @pl.when(jnp.logical_not(has[side]))
-        def _():
-            halo[:, :, side] = jnp.zeros_like(halo[:, :, side])
 
     def body(*accs):
         acc = (accs[:2], accs[2:])
@@ -124,7 +120,7 @@
             cut = (i, slice(None), slice(k * T, (k + 1) * T))
             return terms(ahi.at[cut], alo.at[cut], right_high, right_low)
 
-        def precondition(pairs, c, first):
+        def precondition(pairs, s, c, first):
             for pair in pairs:
                 values = products(
                     [terms(mhi.at[j], mlo.at[j], rhi.at[c, j], rlo.at[c, j]) for j in pair]
@@ -137,9 +133,9 @@
                         x[where] = x[where] + value
                     dhi[c, j], dlo[c, j] = split(value)
                     if j < 2:
-                        dsend[c, 0, j] = value
+                        dsend[s, c, 0, j] = value
                     elif j >= blocks - 2:
-                        dsend[c, 1, j - (blocks - 2)] = value
+                        dsend[s, c, 1, j - (blocks - 2)] = value
 
         def settle(s, c, j, value, keep):
             where = (rows_of(j), cols_of(c))
@@ -155,8 +151,8 @@
                 total = total + jnp.sum((value * value).reshape(T // 8, 8, T), axis=0)
             part[s, c] = total
 
-        def local(s, c):
-            for pair in zip(*((0, 1, *inner[0]), (blocks - 1, blocks - 2, *inner[1]))):
+        def local(s, c, pairs):
+            for pair in pairs:
                 jobs = []
                 for i in pair:
                     job = []
@@ -175,7 +171,7 @@
 
         def halo_copy(s, c, side):
             return pltpu.make_async_remote_copy(
-                src_ref=dsend.at[c, side],
+                src_ref=dsend.at[s, c, side],
                 dst_ref=halo.at[s, c, 1 - side],
                 send_sem=send_sem.at[s, c, side],
                 recv_sem=recv_sem.at[s, c, 1 - side],
@@ -197,13 +193,13 @@
                 def _():
                     halo_copy(s, c, side).wait_send()
 
-        def remote(s, c, keep):
+        def arrive(s, c):
             for side in range(2):
 
                 @pl.when(has[side])
                 def _():
                     pltpu.make_async_remote_copy(
-                        src_ref=dsend.at[c, side],
+                        src_ref=dsend.at[s, c, side],
                         dst_ref=halo.at[s, c, side],
                         send_sem=send_sem.at[s, c, side],
                         recv_sem=recv_sem.at[s, c, side],
@@ -211,6 +207,7 @@
                         device_id_type=MESH,
                     ).wait_recv()
 
+        def remote(s, c, keep):
             for side in range(2):
                 for q in range(2):
                     hhi[side, q], hlo[side, q] = split(halo[s, c, side, q])
@@ -286,56 +283,75 @@
         edge_pairs = ((0, blocks - 1), (1, blocks - 2))
         inner_pairs = tuple(zip(*inner))
 
+        def ready_band(js):
+            for j in js:
+                a_copy(j).wait()
+            for j in js:
+                ahi[j], alo[j] = split(a32[j])
+
         ready_precond(edge)
         for c in range(chunks):
             ready_rhs(edge, c)
-            precondition(edge_pairs, c, True)
+            precondition(edge_pairs, 0, c, True)
             if c == 0:
                 pl.semaphore_wait(
                     barrier, peers + far[0].astype(jnp.int32) + far[1].astype(jnp.int32)
                 )
             send(0, c)
-        ready_precond(inner_flat)
-        for c in range(chunks):
-            ready_rhs(inner_flat, c)
-            precondition(inner_pairs, c, True)
-        for j in (*edge, *inner_flat):
-            a_copy(j).wait()
-            ahi[j], alo[j] = split(a32[j])
-
-        def first_local(c, carry):
-            local(0, c)
-            return carry
-
-        lax.fori_loop(0, chunks, first_local, 0)
+        part[...] = jnp.zeros_like(part)
+        for side in range(2):
+
+            @pl.when(jnp.logical_not(has[side]))
+            def _():
+                halo[:, :, side] = jnp.zeros_like(halo[:, :, side])
+
+        for j in inner_flat:
+            m_copy(j).wait()
+            for c in range(chunks):
+                b_copy(j, c).wait()
+        for j in inner_flat:
+            mhi[j], mlo[j] = split(m32[j])
+        for c in range(chunks):
+            for j in inner_flat:
+                rhi[c, j], rlo[c, j] = split(r[rows_of(j), cols_of(c)])
+            precondition(inner_pairs, 0, c, True)
+        ready_band(band_pairs[0])
+        for n, pair in enumerate(band_pairs):
+            if n + 1 < len(band_pairs):
+                ready_band(band_pairs[n + 1])
+            for c in range(chunks):
+                local(0, c, (pair,))
 
         def unit(u, carry):
             s, c = u // chunks, u % chunks
+            precondition(inner_pairs[:1], s + 1, c, False)
+            arrive(s, c)
             remote(s, c, True)
-            sent(s, c)
-            precondition(edge_pairs, c, False)
+            precondition(inner_pairs[1:], s + 1, c, False)
+            precondition(edge_pairs, s + 1, c, False)
+            sum_line(s, c)
             send(s + 1, c)
-            sum_line(s, c)
-            precondition(inner_pairs, c, False)
-            local(s + 1, c)
-            sum_lines(s, c)
+            local(s + 1, c, band_pairs[::-1])
             return carry
 
         lax.fori_loop(0, (SWEEPS - 1) * chunks, unit, 0)
 
         last = SWEEPS - 1
-        for c in range(chunks):
+        earlier = [(s, c) for s in range(last) for c in range(chunks)]
+        for c in range(chunks):
+            arrive(last, c)
             remote(last, c, False)
             sum_line(last, c)
-            sent(last, c)
-            if c > 0:
-                sum_lines(last, c - 1)
-        sum_lines(last, chunks - 1)
-        for s in range(SWEEPS - 1):
+            if c == 0:
+                for s, other in earlier:
+                    sum_lines(s, other)
+        for c in range(chunks):
+            sum_lines(last, c)
+        for s in range(SWEEPS):
             for c in range(chunks):
-                history[s : s + 1, cols_of(c)] = jnp.sqrt(
-                    summed(s, c) / (rows_n * blocks * T) + 1e-06
-                )
+                sent(s, c)
+        for s, c in earlier:
+            history[s : s + 1, cols_of(c)] = jnp.sqrt(summed(s, c) / (rows_n * blocks * T) + 1e-06)
         grand = jnp.zeros((1, 1), F32)
         roots = []
         for c in range(chunks):
@@ -370,6 +386,22 @@
         overall[...] = jnp.sqrt(grand / (rows_n * blocks * T * rhs_n * rhs.shape[1]) + 1e-06)
 
     pl.run_scoped(body, *([pltpu.ACC(0)((T, T), F32)] * 2), *([pltpu.ACC(1)((T, T), F32)] * 2))
+
+
+def write_out(x, r, history, overall, x_out, r_out, history_out, overall_out, sem, small_sem):
+    height = x.shape[0] // PIECES
+    copies = [
+        pltpu.make_async_copy(history, history_out, small_sem.at[0]),
+        pltpu.make_async_copy(overall, overall_out, small_sem.at[1]),
+    ]
+    for n in range(PIECES):
+        rows = slice(n * height, (n + 1) * height)
+        copies.append(pltpu.make_async_copy(x.at[rows], x_out.at[rows], sem.at[0, n]))
+        copies.append(pltpu.make_async_copy(r.at[rows], r_out.at[rows], sem.at[1, n]))
+    for copy in copies:
+        copy.start()
+    for copy in copies:
+        copy.wait()
 
 
 def shards(rows_n, rhs_n, band_blocks, precond_blocks, right_side):
@@ -386,8 +418,8 @@
         out_shape=(
             vmem((n_rows, n_cols), F32),
             vmem((n_rows, n_cols), F32),
-            jax.ShapeDtypeStruct((SWEEPS, n_cols), F32),
-            jax.ShapeDtypeStruct((1, 128), F32),
+            vmem((SWEEPS, n_cols), F32),
+            vmem((1, 128), F32),
         ),
         in_specs=[pl.BlockSpec(memory_space=pltpu.HBM)] * 3,
         out_specs=[pl.BlockSpec(memory_space=vmem)] * 4,
@@ -402,7 +434,7 @@
             vmem((chunks, blocks, T, T), BF16),
             vmem((chunks, blocks, T, T), BF16),
             vmem((chunks, blocks, T, T), BF16),
-            vmem((chunks, 2, 2, T, T), F32),
+            vmem((SWEEPS, chunks, 2, 2, T, T), F32),
             vmem((SWEEPS, chunks, 2, 2, T, T), F32),
             vmem((2, 2, T, T), BF16),
             vmem((2, 2, T, T), BF16),
@@ -426,10 +458,24 @@
             dma((rhs_n,)),
         ],
         compiler_params=pltpu.CompilerParams(
-            collective_id=0, has_side_effects=True, vmem_limit_bytes=50 * 1024 * 1024
+            collective_id=0, has_side_effects=True, vmem_limit_bytes=54 * 1024 * 1024
         ),
         name="refine",
     )(band_blocks, precond_blocks, right_side)
+    x, r, history, overall = pl.pallas_call(
+        write_out,
+        out_shape=(
+            jax.ShapeDtypeStruct((n_rows, n_cols), F32),
+            jax.ShapeDtypeStruct((n_rows, n_cols), F32),
+            jax.ShapeDtypeStruct((SWEEPS, n_cols), F32),
+            jax.ShapeDtypeStruct((1, 128), F32),
+        ),
+        in_specs=[pl.BlockSpec(memory_space=vmem)] * 4,
+        out_specs=[pl.BlockSpec(memory_space=pltpu.HBM)] * 4,
+        scratch_shapes=[dma((2, PIECES)), dma((2,))],
+        compiler_params=pltpu.CompilerParams(vmem_limit_bytes=1024 * 1024),
+        name="write_out",
+    )(x, r, history, overall)
     return x, r, history, overall[0, 0]
 
 

time: 83.3 us -> 65.6 us (0.79)
  Pallas kernels: 76 us -> 64 us
  local copies, waits for them, and re-layouts: 4.63 us -> 0 us
  between operations: 1.81 us -> 0.8 us
    pallas_call x1, Pallas kernels: 76 us -> 60.6 us  [shards(): pl.pallas_call(functools.partial(kernel, rows_n, rhs_n, blocks), out_shap...]
    unnamed x7 -> x0, local copies, waits for them, and re-layouts: 4.63 us -> none
    pallas_call x0 -> x1, Pallas kernels: none -> 3.39 us  [shards(): pl.pallas_call(write_out, out_shape=(jax.ShapeDtypeStruct((n_rows, n_cols...]
where the time goes in v2:
time: 65.6 us; the launch traced here: 64.8 us
  Pallas kernels  64 us (98%)
  between operations  0.8 us (1%)
    pallas_call x1, Pallas kernels, shards(): pl.pallas_call(functools.partial(kernel, rows_n, rhs_n, blocks), out_shap...  60.6 us
    pallas_call x1, Pallas kernels, shards(): pl.pallas_call(write_out, out_shape=(jax.ShapeDtypeStruct((n_rows, n_cols...  3.39 us

profile of v2, /device:TPU:1, one launch (start us, length us, event | category | flops | bytes accessed | tf_op | source)
XLA Modules:
  0.0 64.8 jit_solution(13245196351629106417)
XLA Ops:
  0.6 60.6 %refine.1 = (f32[2048,512]{1,0:T(8,128)S(1)}, f32[2048,512]{1,0:T(8,128)S(1)}, f32[3,512]{1,0:T(4,128)S(1)}, f32[1,128]{1,0:T(1,128)S(1)}) custom-call(f32[8,256,1280]{2,1,0:T(8,128)} %band.1, f32[8,256,256]{2,1,0:T(8,128)} %precond.1, f32[2048,512]{1,0:T(8,128)} %rhs.1), custom_call_target="tpu_custom_call" | custom-call | tf_op jit(solution)/shard_map/refine/pallas_call | solution.py:416
  61.2 3.4 %write_out.1 = (f32[2048,512]{1,0:T(8,128)}, f32[2048,512]{1,0:T(8,128)}, f32[3,512]{1,0:T(4,128)}, f32[1,128]{1,0:T(1,128)}) custom-call(f32[2048,512]{1,0:T(8,128)S(1)} %get-tuple-element.12.x, f32[2048,512]{1,0:T(8,128)S(1)} %get-tuple-element.13.r, f32[3,512]{1,0:T(4,128)S(1)} %get-tuple-element.14.history, f32[1,128]{1,0:T(1,128)S(1)} %get-tuple-element.15.overall), custom_call_target="tpu_custom_call" | custom-call | tf_op jit(solution)/shard_map/write_out/pallas_call | solution.py:465

commit v3 on v2

--- a/solution.py
+++ b/solution.py
@@ -25,6 +25,7 @@
     band, precond, rhs,
     x, r, history, overall,
     a32, m32, ahi, alo, mhi, mlo, rhi, rlo, dhi, dlo, dsend, halo, hhi, hlo, part, msg, p1, mid, p2, zmsg, zbuf,
+    ready, last_msg, last_all, last_send, last_recv,
     a_sem, m_sem, b_sem, send_sem, recv_sem, p1_send, p1_recv, p2_send, p2_recv, z_send, z_recv,
 ):
     me = lax.axis_index("rows")
@@ -35,6 +36,7 @@
     beside = (me - 1, me + 1)
     far = ((spot == 0) & has[0], (spot == LINE - 1) & has[1])
     chunks = rhs.shape[1] // T
+    assert chunks == 2
     edge = (0, 1, blocks - 1, blocks - 2)
     inner = tuple(range(2, blocks // 2)), tuple(range(blocks - 3, blocks // 2 - 1, -1))
     inner_flat = tuple(j for pair in zip(*inner) for j in pair)
@@ -62,16 +64,16 @@
         m_copy(j).start()
     for c in range(chunks):
         for j in edge:
-            b_copy(j, c).start()
+            b_copy(j, c).start(priority=min(c, 1))
     for j in inner_flat:
-        m_copy(j).start()
+        m_copy(j).start(priority=1)
     for c in range(chunks):
         for j in inner_flat:
-            b_copy(j, c).start()
+            b_copy(j, c).start(priority=1)
     band_pairs = tuple(zip((0, 1, *inner[0]), (blocks - 1, blocks - 2, *inner[1])))
     for pair in band_pairs:
         for j in pair:
-            a_copy(j).start()
+            a_copy(j).start(priority=1)
 
     barrier = pltpu.get_barrier_semaphore()
     for k in range(1, LINE):
@@ -298,6 +300,10 @@
                     barrier, peers + far[0].astype(jnp.int32) + far[1].astype(jnp.int32)
                 )
             send(0, c)
+        for k in range(1, LINE):
+            pl.semaphore_signal(
+                ready, inc=1, device_id={"rows": line * LINE + (spot + k) % LINE}, device_id_type=MESH
+            )
         part[...] = jnp.zeros_like(part)
         for side in range(2):
 
@@ -320,7 +326,8 @@
             if n + 1 < len(band_pairs):
                 ready_band(band_pairs[n + 1])
             for c in range(chunks):
-                local(0, c, (pair,))
+                if c == 0 or pair in edge_pairs:
+                    local(0, c, (pair,))
 
         def unit(u, carry):
             s, c = u // chunks, u % chunks
@@ -331,35 +338,47 @@
             precondition(edge_pairs, s + 1, c, False)
             sum_line(s, c)
             send(s + 1, c)
-            local(s + 1, c, band_pairs[::-1])
+            local((u + 1) // chunks, 1 - c, inner_pairs[::-1])
+            local(s + 1, c, edge_pairs[::-1])
             return carry
 
         lax.fori_loop(0, (SWEEPS - 1) * chunks, unit, 0)
+
+        def last_copy(k):
+            return pltpu.make_async_remote_copy(
+                src_ref=last_msg,
+                dst_ref=last_all.at[k],
+                send_sem=last_send.at[k],
+                recv_sem=last_recv.at[k],
+                device_id={"rows": (me + k) % rows_n},
+                device_id_type=MESH,
+            )
 
         last = SWEEPS - 1
         earlier = [(s, c) for s in range(last) for c in range(chunks)]
+        local(last, chunks - 1, inner_pairs)
         for c in range(chunks):
             arrive(last, c)
             remote(last, c, False)
-            sum_line(last, c)
+            last_msg[:, cols_of(c)] = jnp.sum(part[last, c], axis=0, keepdims=True)
             if c == 0:
+                pl.semaphore_wait(ready, LINE - 1)
                 for s, other in earlier:
                     sum_lines(s, other)
-        for c in range(chunks):
-            sum_lines(last, c)
+        for k in range(1, rows_n):
+            last_copy(k).start()
         for s in range(SWEEPS):
             for c in range(chunks):
                 sent(s, c)
         for s, c in earlier:
             history[s : s + 1, cols_of(c)] = jnp.sqrt(summed(s, c) / (rows_n * blocks * T) + 1e-06)
-        grand = jnp.zeros((1, 1), F32)
-        roots = []
-        for c in range(chunks):
-            total = summed(last, c)
-            grand = grand + jnp.sum(total, axis=1, keepdims=True)
-            root = jnp.sqrt(total / (rows_n * blocks * T) + 1e-06)
-            history[last : last + 1, cols_of(c)] = root
-            roots.append(root)
+        last_all[0] = last_msg[...]
+        for k in range(1, rows_n):
+            last_copy(k).wait()
+        total = jnp.sum(last_all[...], axis=0)
+        root = jnp.sqrt(total / (rows_n * blocks * T) + 1e-06)
+        history[last : last + 1] = root
+        grand = jnp.sum(total, axis=1, keepdims=True)
         zmsg[...] = jnp.broadcast_to(grand, zmsg.shape)
 
         def z_copy(k):
@@ -374,11 +393,9 @@
 
         for k in range(1, rhs_n):
             z_copy(k).start()
-        for c in range(chunks):
-            inverse = 1.0 / roots[c]
-            for j in range(blocks):
-                where = (rows_of(j), cols_of(c))
-                r[where] = r[where] * inverse
+        inverse = 1.0 / root
+        for j in range(blocks):
+            r[rows_of(j)] = r[rows_of(j)] * inverse
         grand = zmsg[...]
         for k in range(1, rhs_n):
             z_copy(k).wait()
@@ -445,6 +462,11 @@
             vmem((SWEEPS, chunks, rows_n // LINE, 1, T), F32),
             vmem((1, 128), F32),
             vmem((rhs_n, 1, 128), F32),
+            pltpu.SemaphoreType.REGULAR,
+            vmem((1, n_cols), F32),
+            vmem((rows_n, 1, n_cols), F32),
+            dma((rows_n,)),
+            dma((rows_n,)),
             dma((blocks,)),
             dma((blocks,)),
             dma((blocks, chunks)),

time: 65.6 us -> 62.6 us (0.954); the launches traced: 64.8 us -> 62.5 us
  Pallas kernels: 64 us -> 61.7 us
    pallas_call x1, Pallas kernels: 60.6 us -> 58.3 us  [shards(): pl.pallas_call(functools.partial(kernel, rows_n, rhs_n, blocks), out_shap...]
where the time goes in v3:
time: 62.6 us; the launch traced here: 62.5 us
  Pallas kernels  61.7 us (99%)
  between operations  0.8 us (1%)
    pallas_call x1, Pallas kernels, shards(): pl.pallas_call(functools.partial(kernel, rows_n, rhs_n, blocks), out_shap...  58.3 us
    pallas_call x1, Pallas kernels, shards(): pl.pallas_call(write_out, out_shape=(jax.ShapeDtypeStruct((n_rows, n_cols...  3.39 us

profile of v3, /device:TPU:1, one launch (start us, length us, event | category | flops | bytes accessed | tf_op | source)
XLA Modules:
  0.0 62.5 jit_solution(2363732085727974409)
XLA Ops:
  0.6 58.3 %refine.1 = (f32[2048,512]{1,0:T(8,128)S(1)}, f32[2048,512]{1,0:T(8,128)S(1)}, f32[3,512]{1,0:T(4,128)S(1)}, f32[1,128]{1,0:T(1,128)S(1)}) custom-call(f32[8,256,1280]{2,1,0:T(8,128)} %band.1, f32[8,256,256]{2,1,0:T(8,128)} %precond.1, f32[2048,512]{1,0:T(8,128)} %rhs.1), custom_call_target="tpu_custom_call" | custom-call | tf_op jit(solution)/shard_map/refine/pallas_call | solution.py:433
  58.9 3.4 %write_out.1 = (f32[2048,512]{1,0:T(8,128)}, f32[2048,512]{1,0:T(8,128)}, f32[3,512]{1,0:T(4,128)}, f32[1,128]{1,0:T(1,128)}) custom-call(f32[2048,512]{1,0:T(8,128)S(1)} %get-tuple-element.12.x, f32[2048,512]{1,0:T(8,128)S(1)} %get-tuple-element.13.r, f32[3,512]{1,0:T(4,128)S(1)} %get-tuple-element.14.history, f32[1,128]{1,0:T(1,128)S(1)} %get-tuple-element.15.overall), custom_call_target="tpu_custom_call" | custom-call | tf_op jit(solution)/shard_map/write_out/pallas_call | solution.py:487

commit v4 on v3

--- a/solution.py
+++ b/solution.py
@@ -25,7 +25,7 @@
     band, precond, rhs,
     x, r, history, overall,
     a32, m32, ahi, alo, mhi, mlo, rhi, rlo, dhi, dlo, dsend, halo, hhi, hlo, part, msg, p1, mid, p2, zmsg, zbuf,
-    ready, last_msg, last_all, last_send, last_recv,
+    ready, all_ready, last_msg, last_all, last_send, last_recv,
     a_sem, m_sem, b_sem, send_sem, recv_sem, p1_send, p1_recv, p2_send, p2_recv, z_send, z_recv,
 ):
     me = lax.axis_index("rows")
@@ -350,7 +350,22 @@
                 dst_ref=last_all.at[k],
                 send_sem=last_send.at[k],
                 recv_sem=last_recv.at[k],
-                device_id={"rows": (me + k) % rows_n},
+                device_id={
+                    "rows": (line + k // LINE) % lines * LINE + (spot + k % LINE) % LINE
+                },
+                device_id_type=MESH,
+            )
+
+        def z_copy(n):
+            return pltpu.make_async_remote_copy(
+                src_ref=zmsg,
+                dst_ref=zbuf.at[n],
+                send_sem=z_send.at[n],
+                recv_sem=z_recv.at[n],
+                device_id={
+                    "rows": (line + n // rhs_n) % lines * LINE + spot,
+                    "rhs": (z + n % rhs_n) % rhs_n,
+                },
                 device_id_type=MESH,
             )
 
@@ -363,43 +378,39 @@
             last_msg[:, cols_of(c)] = jnp.sum(part[last, c], axis=0, keepdims=True)
             if c == 0:
                 pl.semaphore_wait(ready, LINE - 1)
+                for k in range(1, rhs_n):
+                    pl.semaphore_signal(
+                        all_ready, inc=1, device_id={"rhs": (z + k) % rhs_n}, device_id_type=MESH
+                    )
                 for s, other in earlier:
                     sum_lines(s, other)
         for k in range(1, rows_n):
             last_copy(k).start()
+        last_all[0] = last_msg[...]
+        pl.semaphore_wait(all_ready, rhs_n - 1)
+        for k in range(1, LINE):
+            last_copy(k).wait()
+        grand = jnp.sum(jnp.sum(last_all[:LINE], axis=0), axis=1, keepdims=True)
+        zmsg[...] = jnp.broadcast_to(grand, zmsg.shape)
+        for n in range(1, lines * rhs_n):
+            z_copy(n).start()
         for s in range(SWEEPS):
             for c in range(chunks):
                 sent(s, c)
         for s, c in earlier:
             history[s : s + 1, cols_of(c)] = jnp.sqrt(summed(s, c) / (rows_n * blocks * T) + 1e-06)
-        last_all[0] = last_msg[...]
-        for k in range(1, rows_n):
+        for k in range(LINE, rows_n):
             last_copy(k).wait()
         total = jnp.sum(last_all[...], axis=0)
         root = jnp.sqrt(total / (rows_n * blocks * T) + 1e-06)
         history[last : last + 1] = root
-        grand = jnp.sum(total, axis=1, keepdims=True)
-        zmsg[...] = jnp.broadcast_to(grand, zmsg.shape)
-
-        def z_copy(k):
-            return pltpu.make_async_remote_copy(
-                src_ref=zmsg,
-                dst_ref=zbuf.at[k],
-                send_sem=z_send.at[k],
-                recv_sem=z_recv.at[k],
-                device_id={"rhs": (z + k) % rhs_n},
-                device_id_type=MESH,
-            )
-
-        for k in range(1, rhs_n):
-            z_copy(k).start()
         inverse = 1.0 / root
         for j in range(blocks):
             r[rows_of(j)] = r[rows_of(j)] * inverse
         grand = zmsg[...]
-        for k in range(1, rhs_n):
-            z_copy(k).wait()
-            grand = grand + zbuf[k]
+        for n in range(1, lines * rhs_n):
+            z_copy(n).wait()
+            grand = grand + zbuf[n]
         overall[...] = jnp.sqrt(grand / (rows_n * blocks * T * rhs_n * rhs.shape[1]) + 1e-06)
 
     pl.run_scoped(body, *([pltpu.ACC(0)((T, T), F32)] * 2), *([pltpu.ACC(1)((T, T), F32)] * 2))
@@ -461,7 +472,8 @@
             vmem((SWEEPS, chunks, 1, T), F32),
             vmem((SWEEPS, chunks, rows_n // LINE, 1, T), F32),
             vmem((1, 128), F32),
-            vmem((rhs_n, 1, 128), F32),
+            vmem((rows_n // LINE * rhs_n, 1, 128), F32),
+            pltpu.SemaphoreType.REGULAR,
             pltpu.SemaphoreType.REGULAR,
             vmem((1, n_cols), F32),
             vmem((rows_n, 1, n_cols), F32),
@@ -476,8 +488,8 @@
             dma((SWEEPS, chunks, LINE)),
             dma((SWEEPS, chunks, rows_n // LINE)),
             dma((SWEEPS, chunks, rows_n // LINE)),
-            dma((rhs_n,)),
-            dma((rhs_n,)),
+            dma((rows_n // LINE * rhs_n,)),
+            dma((rows_n // LINE * rhs_n,)),
         ],
         compiler_params=pltpu.CompilerParams(
             collective_id=0, has_side_effects=True, vmem_limit_bytes=54 * 1024 * 1024

time: 62.6 us -> 62.7 us (level)
  no operation moved by 1% of the time
where the time goes in v4:
time: 62.7 us; the launch traced here: 62.6 us
  Pallas kernels  61.8 us (99%)
  between operations  0.8 us (1%)
    pallas_call x1, Pallas kernels, shards(): pl.pallas_call(functools.partial(kernel, rows_n, rhs_n, blocks), out_shap...  58.4 us
    pallas_call x1, Pallas kernels, shards(): pl.pallas_call(write_out, out_shape=(jax.ShapeDtypeStruct((n_rows, n_cols...  3.39 us

profile of v4, /device:TPU:1, one launch (start us, length us, event | category | flops | bytes accessed | tf_op | source)
XLA Modules:
  0.0 62.6 jit_solution(1152867609455517781)
XLA Ops:
  0.6 58.4 %refine.1 = (f32[2048,512]{1,0:T(8,128)S(1)}, f32[2048,512]{1,0:T(8,128)S(1)}, f32[3,512]{1,0:T(4,128)S(1)}, f32[1,128]{1,0:T(1,128)S(1)}) custom-call(f32[8,256,1280]{2,1,0:T(8,128)} %band.1, f32[8,256,256]{2,1,0:T(8,128)} %precond.1, f32[2048,512]{1,0:T(8,128)} %rhs.1), custom_call_target="tpu_custom_call" | custom-call | tf_op jit(solution)/shard_map/refine/pallas_call | solution.py:444
  59.0 3.4 %write_out.1 = (f32[2048,512]{1,0:T(8,128)}, f32[2048,512]{1,0:T(8,128)}, f32[3,512]{1,0:T(4,128)}, f32[1,128]{1,0:T(1,128)}) custom-call(f32[2048,512]{1,0:T(8,128)S(1)} %get-tuple-element.12.x, f32[2048,512]{1,0:T(8,128)S(1)} %get-tuple-element.13.r, f32[3,512]{1,0:T(4,128)S(1)} %get-tuple-element.14.history, f32[1,128]{1,0:T(1,128)S(1)} %get-tuple-element.15.overall), custom_call_target="tpu_custom_call" | custom-call | tf_op jit(solution)/shard_map/write_out/pallas_call | solution.py:499
